TPU v7x, 256 devices: a whole 4x4x8 slice. The times are simulated.
256 devices in a mesh: rows: 32 (over z, y), cols: 8 (over x, core).
Axes of the slice: x: 4, y: 4, z: 8, core: 2. Of those that a mesh axis runs over, the one named last changes fastest.
Arguments:
- weight_up: bfloat16 [12288, 49152], P('rows', 'cols'), may hold values from -0.109375 to 0.109375
- low_up: bfloat16 [12288, 64], P('rows'), may hold values from -0.0546875 to 0.0546875
- high_up: bfloat16 [64, 49152], P(None, 'cols'), may hold values from -0.75 to 0.75
- norm_train: float32 [12288], P(('rows', 'cols')), may hold values from 0.25 to 1.75
- norm_step: float32 [12288], P(('rows', 'cols')), may hold values from -0.3 to 0.3
Outputs:
- serve_up: bfloat16 [12288, 49152], P(None, ('cols', 'rows'))
- scale_up: float32 [49152], P(('cols', 'rows'))
- serve_norm: bfloat16 [12288], replicated
All inputs are finite; a program needn't handle non-finite values.
Results may differ from a plain program's by a relative error of at most 0.0004.
Values may be sent and summed in bfloat16 or wider, within the bound.
A program may use at most 64 MiB of HBM per device.

v0:
```python
import jax
import jax.numpy as jnp
from jax import lax
from jax.sharding import Mesh
from jax.sharding import PartitionSpec as P

ROWS = ("rows_0", "rows_1")
ROWS_COLS = ("rows_0", "rows_1", "cols_0", "cols_1")
COLS = ("cols_0", "cols_1")
COLS_ROWS = ("cols_0", "cols_1", "rows_0", "rows_1")
mix_rate = 0.5


def copy_for_each(x, axis):
    copies = jnp.broadcast_to(x, (lax.axis_size(axis), *x.shape))
    return lax.all_to_all(copies, axis, split_axis=0, concat_axis=0, tiled=True)


def of_everyone(x, axis):
    return copy_for_each(x, axis).sum(axis=0)


def joined_along(pieces, dim):
    shape = list(pieces.shape[1:])
    shape[dim] *= pieces.shape[0]
    return jnp.moveaxis(pieces, 0, dim).reshape(shape)


def stacked_from(x, axes, sequence):
    pieces = x[None]
    for k in sequence:
        pieces = lax.all_gather(pieces, axes[k], axis=0, tiled=True)
    block = [lax.axis_size(axes[k]) for k in reversed(sequence)]
    pieces = pieces.reshape(*block, *x.shape)
    turned = sorted(range(len(sequence)), key=lambda place: sequence[len(sequence) - 1 - place])
    return pieces.transpose(*turned, *range(len(sequence), pieces.ndim)).reshape(-1, *x.shape)


def gathered_by_axis(x, axes, sequence, dim):
    return joined_along(stacked_from(x, axes, sequence), dim)


def per_device(weight_up, low_up, high_up, norm_train, norm_step):
    fresh_up = weight_up.astype(jnp.float32) + mix_rate * jnp.dot(
        low_up, high_up, preferred_element_type=jnp.float32
    )
    total_up = of_everyone(jnp.sum(fresh_up * fresh_up, axis=0), ROWS)
    scale_up = jnp.sqrt(total_up)
    narrow_up = (fresh_up / scale_up).astype(jnp.bfloat16)
    serve_up = lax.all_to_all(narrow_up, ROWS, split_axis=1, concat_axis=0, tiled=True)
    place = lax.axis_index(ROWS)
    scale_up = lax.dynamic_slice_in_dim(scale_up, place * serve_up.shape[1], serve_up.shape[1])
    serve_norm = gathered_by_axis(
        (norm_train + norm_step).astype(jnp.bfloat16), ROWS_COLS, (1, 0, 2, 3), 0
    )
    return (serve_up, scale_up, serve_norm)


def solution(mesh):
    split = Mesh(mesh.devices.reshape(8, 4, 4, 2), ("rows_0", "rows_1", "cols_0", "cols_1"))
    in_specs = (P(ROWS, COLS), P(ROWS, None), P(None, COLS), P(ROWS_COLS), P(ROWS_COLS))
    out_specs = (P(None, COLS_ROWS), P(COLS_ROWS), P())
    return jax.shard_map(
        per_device, mesh=split, in_specs=in_specs, out_specs=out_specs, check_vma=False
    )
```

profile of v0, /device:TPU:1, one launch (start us, length us, event | category | flops | bytes accessed | tf_op | source)
XLA Modules:
  0.0 198.1 jit_solution(16278709822635123350)
XLA Ops:
  0.6 0.0 copy-start
  0.6 1.1 copy-done
  1.8 8.0 %multiply_reduce_fusion = (f32[6144]{0:T(1024)S(1)}, f32[384,6144]{1,0:T(8,128)}) fusion(bf16[384,64]{0,1:T(8,128)(2,1)} %param.6, bf16[64,6144]{1,0:T(8,128)(2,1)S(1)} %copy-done, bf16[384,6144]{1,0:T(8,128)(2,1)} %param.5), kind=kOutput, calls=%fused_computation.1 | convolution fusion | flops 313780224 | bytes 15015936 | tf_op jit(solution)/shard_map/dot_general | solution.py:44
  9.8 0.4 broadcast_in_dim.7
  10.2 32.9 %all_to_all.25 = f32[32,1,6144]{2,1,0:T(1,128)S(1)} all-to-all(f32[32,1,6144]{2,1,0:T(1,128)S(1)} %broadcast_in_dim.7), channel_id=1, replica_groups=mesh['rows_0'=8,'rows_1'=4,'cols_0'=4,'cols_1'=2] {'rows_0','rows_1'}, dimensions={0} | all-to-all | bytes 1572864 | tf_op jit(solution)/shard_map/all_to_all | solution.py:16
  43.1 0.5 reduce_sum.19
  43.6 6.8 %divide_convert_fusion = bf16[384,6144]{1,0:T(8,128)(2,1)} fusion(f32[384,6144]{1,0:T(8,128)} %get-tuple-element.4, f32[6144]{0:T(1024)S(1)} %sqrt.7), kind=kLoop, calls=%fused_computation | loop fusion | flops 4718592 | bytes 14180352 | tf_op jit(solution)/shard_map/convert_element_type | solution.py:49
  50.4 6.7 %copy.20 = bf16[384,6144]{0,1:T(8,128)(2,1)} copy(bf16[384,6144]{1,0:T(8,128)(2,1)} %divide_convert_fusion) | data formatting | bytes 9437184 | tf_op jit(solution)/shard_map/convert_element_type | solution.py:49
  57.2 5.9 %all-to-all-start.1 = ((bf16[384,32,192]{0,2,1:T(8,128)(2,1)}), bf16[384,32,192]{0,2,1:T(8,128)(2,1)}, u32[]{:S(2)}, u32[]{:S(2)}) async-start(bf16[384,32,192]{0,2,1:T(8,128)(2,1)} %bitcast.11), calls=%async_computation.1 | async-start | bytes 9437184 | tf_op jit(solution)/shard_map/all_to_all | solution.py:50
  63.1 0.0 copy-done.3
  63.1 0.6 dynamic-slice
  64.3 0.0 copy-done.1
  64.3 0.0 copy-done.2
  64.4 0.2 dynamic-update-slice
  64.6 12.9 %all-reduce = bf16[192]{0:T(256)(128)(2,1)S(1)} all-reduce(bf16[192]{0:T(256)(128)(2,1)S(1)} %dynamic-update-slice), channel_id=2, replica_groups=mesh['rows_0'=8,'rows_1'=4,'cols_0'=4,'cols_1'=2] {'rows_1'}, use_global_device_ids=true, to_apply=%add | all-reduce | flops 192 | bytes 768
  77.6 0.1 reshape.24
  77.6 95.8 %all-gather.1 = bf16[8,4,48]{2,1,0:T(4,128)(2,1)S(1)} all-gather(bf16[1,4,48]{2,1,0:T(4,128)(2,1)S(1)} %reshape.24), channel_id=1, replica_groups=mesh['rows_0'=8,'rows_1'=4,'cols_0'=4,'cols_1'=2] {'rows_0'}, dimensions={0}, use_global_device_ids=true | all-gather | bytes 3456 | tf_op jit(solution)/shard_map/all_gather | solution.py:32
  173.4 9.6 %all_gather.14 = bf16[128,48]{1,0:T(8,128)(2,1)S(1)} all-gather(bf16[32,48]{1,0:T(8,128)(2,1)S(1)} %bitcast.14), channel_id=1, replica_groups=mesh['rows_0'=8,'rows_1'=4,'cols_0'=4,'cols_1'=2] {'cols_0'}, dimensions={0}, use_global_device_ids=true | all-gather | bytes 15360 | tf_op jit(solution)/shard_map/all_gather | solution.py:32
  183.0 8.3 %all_gather.15 = bf16[256,48]{1,0:T(8,128)(2,1)S(1)} all-gather(bf16[128,48]{1,0:T(8,128)(2,1)S(1)} %all_gather.14), channel_id=1, replica_groups=mesh['rows_0'=8,'rows_1'=4,'cols_0'=4,'cols_1'=2] {'cols_1'}, dimensions={0}, use_global_device_ids=true | all-gather | bytes 36864 | tf_op jit(solution)/shard_map/all_gather | solution.py:32
  191.3 0.1 copy.22
  191.4 0.7 reshape_reshape.3
  192.1 0.6 dynamic_slice.3
  192.8 0.0 all-to-all-done.1
  192.8 5.3 %copy.24 = bf16[32,24,8,384]{3,2,0,1:T(8,128)(2,1)} copy(bf16[32,24,8,384]{3,2,1,0:T(8,128)(2,1)} %bitcast.7) | data formatting | bytes 9437184 | tf_op jit(solution)/shard_map/all_to_all | solution.py:50
  (6 shorter events, 0.0 us)
Async XLA Ops:
  0.6 1.1 copy-start
  50.4 12.7 %copy-start.3 = (u32[256]{0:T(256)S(1)}, u32[256]{0:T(256)}, u32[]{:S(2)}) copy-start(u32[256]{0:T(256)} %constant.26) | copy-start | bytes 3076
  50.4 13.9 %copy-start.1 = (f32[48]{0:T(128)S(1)}, f32[48]{0:T(128)}, u32[]{:S(2)}) copy-start(f32[48]{0:T(128)} %param.8) | copy-start | bytes 580
  50.4 13.9 %copy-start.2 = (f32[48]{0:T(128)S(1)}, f32[48]{0:T(128)}, u32[]{:S(2)}) copy-start(f32[48]{0:T(128)} %param.9) | copy-start | bytes 580
  57.2 135.6 %all-to-all-start.1 = ((bf16[384,32,192]{0,2,1:T(8,128)(2,1)}), bf16[384,32,192]{0,2,1:T(8,128)(2,1)}, u32[]{:S(2)}, u32[]{:S(2)}) async-start(bf16[384,32,192]{0,2,1:T(8,128)(2,1)} %bitcast.11), calls=%async_computation.1 | async-start | bytes 9437184 | tf_op jit(solution)/shard_map/all_to_all | solution.py:50
where the time goes:
time: 199 us; the launch traced here: 198 us
  blocking collectives  160 us (80%)
  local copies, waits for them, and re-layouts  16 us (8%)
  matrix products  8.02 us (4%)
  other arithmetic  7.29 us (4%)
  starting transfers between devices  5.9 us (3%)
    all_gather x3, blocking collectives, stacked_from(): pieces = lax.all_gather(pieces, axes[k], axis=0, tiled=True)  114 us
    all_to_all x1, blocking collectives, copy_for_each(): return lax.all_to_all(copies, axis, split_axis=0, concat_axis=0, tiled=True)  32.9 us
    unnamed x1, blocking collectives  12.9 us
    dot_general x1, matrix products, per_device(): jnp.dot(low_up, high_up, preferred_element_type=jnp.float32)  8.02 us
    convert_element_type x1, other arithmetic, per_device(): narrow_up = (fresh_up / scale_up).astype(jnp.bfloat16)  6.83 us
    convert_element_type x1, local copies, waits for them, and re-layouts, per_device(): narrow_up = (fresh_up / scale_up).astype(jnp.bfloat16)  6.75 us
    all_to_all x1, starting transfers between devices, per_device(): lax.all_to_all(narrow_up, ROWS, split_axis=1, concat_axis=0, tiled=True)  5.9 us
    all_to_all x1, local copies, waits for them, and re-layouts, per_device(): lax.all_to_all(narrow_up, ROWS, split_axis=1, concat_axis=0, tiled=True)  5.32 us
  transfers between devices with their start and end apart: 1, of which 0 were waited for; matrix products, arithmetic and copies ran while one was open for 1% of the time, Pallas kernels for 0%

commit v1 on v0

--- a/solution.py
+++ b/solution.py
@@ -29,7 +29,9 @@
 def stacked_from(x, axes, sequence):
     pieces = x[None]
     for k in sequence:
-        pieces = lax.all_gather(pieces, axes[k], axis=0, tiled=True)
+        pieces = jnp.concatenate(
+            lax.all_to_all(jnp.stack([pieces] * lax.axis_size(axes[k])), axes[k], 0, 0), axis=0
+        )
     block = [lax.axis_size(axes[k]) for k in reversed(sequence)]
     pieces = pieces.reshape(*block, *x.shape)
     turned = sorted(range(len(sequence)), key=lambda place: sequence[len(sequence) - 1 - place])

time: 199 us -> 204 us (1.025)
  the two profiles are of different devices: /device:TPU:1 before, /device:TPU:11 now
where the time goes in v1:
time: 204 us; the launch traced here: 203 us
  waiting for transfers between devices  126 us (62%)
  starting transfers between devices  22.9 us (11%)
  blocking collectives  21.6 us (11%)
  local copies, waits for them, and re-layouts  15.8 us (8%)
  other arithmetic  8.68 us (4%)
  matrix products  8.04 us (4%)
    all_to_all x1, waiting for transfers between devices, per_device(): lax.all_to_all(narrow_up, ROWS, split_axis=1, concat_axis=0, tiled=True)  108 us
    all_to_all x2, blocking collectives, stacked_from(): lax.all_to_all(jnp.stack([pieces] * lax.axis_size(axes[k])), axes[k], 0, 0)  21.6 us
    all_to_all x1, waiting for transfers between devices, copy_for_each(): return lax.all_to_all(copies, axis, split_axis=0, concat_axis=0, tiled=True)  17.4 us
    all_to_all x2, starting transfers between devices, stacked_from(): lax.all_to_all(jnp.stack([pieces] * lax.axis_size(axes[k])), axes[k], 0, 0)  13.1 us
    dot_general x1, matrix products, per_device(): jnp.dot(low_up, high_up, preferred_element_type=jnp.float32)  8.04 us
    convert_element_type x1, other arithmetic, per_device(): narrow_up = (fresh_up / scale_up).astype(jnp.bfloat16)  6.83 us
    convert_element_type x1, local copies, waits for them, and re-layouts, per_device(): narrow_up = (fresh_up / scale_up).astype(jnp.bfloat16)  6.69 us
    all_to_all x1, local copies, waits for them, and re-layouts, per_device(): lax.all_to_all(narrow_up, ROWS, split_axis=1, concat_axis=0, tiled=True)  5.32 us
  transfers between devices with their start and end apart: 4, of which 2 were waited for; matrix products, arithmetic and copies ran while one was open for 12% of the time, Pallas kernels for 0%

profile of v1, /device:TPU:11, one launch (start us, length us, event | category | flops | bytes accessed | tf_op | source)
XLA Modules:
  0.0 203.4 jit_solution(12660332482941651942)
XLA Ops:
  0.6 0.0 copy-start
  0.6 0.7 add_convert_fusion
  1.4 7.1 %all_to_all.45 = bf16[4,1,48]{2,1,0:T(2,128)(2,1)S(1)} all-to-all(bf16[4,1,48]{2,1,0:T(2,128)(2,1)S(1)} %stack.12), channel_id=1, replica_groups=mesh['rows_0'=8,'rows_1'=4,'cols_0'=4,'cols_1'=2] {'rows_1'}, dimensions={0} | all-to-all | bytes 768 | tf_op jit(solution)/shard_map/all_to_all | solution.py:33
  8.5 14.6 %all_to_all.46 = bf16[8,4,48]{2,1,0:T(4,128)(2,1)S(1)} all-to-all(bf16[8,4,48]{2,1,0:T(4,128)(2,1)S(1)} %stack.13), channel_id=1, replica_groups=mesh['rows_0'=8,'rows_1'=4,'cols_0'=4,'cols_1'=2] {'rows_0'}, dimensions={0} | all-to-all | bytes 6144 | tf_op jit(solution)/shard_map/all_to_all | solution.py:33
  23.1 0.7 reshape.22
  23.8 4.3 %all-to-all-start.4 = ((bf16[4,2,768]{2,1,0:T(2,128)(2,1)}), bf16[4,2,768]{2,1,0:T(2,128)(2,1)S(1)}, u32[]{:S(2)}, u32[]{:S(2)}) async-start(bf16[4,2,768]{2,1,0:T(2,128)(2,1)} %reshape.22), calls=%async_computation.4 | async-start | bytes 24576 | tf_op jit(solution)/shard_map/all_to_all | solution.py:33
  28.0 8.0 %multiply_reduce_fusion = (f32[6144]{0:T(1024)S(1)}, f32[384,6144]{1,0:T(8,128)}) fusion(bf16[384,64]{0,1:T(8,128)(2,1)} %param.6, bf16[64,6144]{1,0:T(8,128)(2,1)S(1)} %copy-done, bf16[384,6144]{1,0:T(8,128)(2,1)} %param.5), kind=kOutput, calls=%fused_computation.1 | convolution fusion | flops 313780224 | bytes 15015936 | tf_op jit(solution)/shard_map/dot_general | solution.py:46
  36.1 1.3 broadcast_in_dim.4
  37.4 4.7 %all-to-all-start = ((f32[32,1,6144]{2,1,0:T(1,128)}), f32[32,1,6144]{2,1,0:T(1,128)S(1)}, u32[]{:S(2)}, u32[]{:S(2)}) async-start(f32[32,1,6144]{2,1,0:T(1,128)} %broadcast_in_dim.4), calls=%async_computation | async-start | bytes 1572864 | tf_op jit(solution)/shard_map/all_to_all | solution.py:16
  42.1 0.1 reshape.23
  42.2 0.1 copy.33
  42.3 0.6 pad_maximum_fusion
  42.9 17.4 %all-to-all-done = f32[32,1,6144]{2,1,0:T(1,128)S(1)} async-done(((f32[32,1,6144]{2,1,0:T(1,128)}), f32[32,1,6144]{2,1,0:T(1,128)S(1)}, u32[]{:S(2)}, u32[]{:S(2)}) %all-to-all-start) | async-done | bytes 786464 | tf_op jit(solution)/shard_map/all_to_all | solution.py:16
  60.3 8.8 %all-to-all-start.5 = ((bf16[2,128,48]{1,2,0:T(8,128)(2,1)}), bf16[2,128,48]{1,2,0:T(8,128)(2,1)S(1)}, u32[]{:S(2)}, u32[]{:S(2)}) async-start(bf16[2,128,48]{1,2,0:T(8,128)(2,1)} %pad_maximum_fusion), calls=%async_computation.5 | async-start | bytes 49152 | tf_op jit(solution)/shard_map/all_to_all | solution.py:33
  69.1 0.5 reduce_sum.19
  69.6 6.8 %divide_convert_fusion = bf16[384,6144]{1,0:T(8,128)(2,1)} fusion(f32[384,6144]{1,0:T(8,128)} %get-tuple-element.4, f32[6144]{0:T(1024)S(1)} %sqrt.7), kind=kLoop, calls=%fused_computation | loop fusion | flops 4718592 | bytes 14180352 | tf_op jit(solution)/shard_map/convert_element_type | solution.py:51
  76.4 6.7 %copy.31 = bf16[384,6144]{0,1:T(8,128)(2,1)} copy(bf16[384,6144]{1,0:T(8,128)(2,1)} %divide_convert_fusion) | data formatting | bytes 9437184 | tf_op jit(solution)/shard_map/convert_element_type | solution.py:51
  83.1 5.1 %all-to-all-start.1 = ((bf16[384,32,192]{0,2,1:T(8,128)(2,1)}), bf16[384,32,192]{0,2,1:T(8,128)(2,1)}, u32[]{:S(2)}, u32[]{:S(2)}) async-start(bf16[384,32,192]{0,2,1:T(8,128)(2,1)} %bitcast.14), calls=%async_computation.1 | async-start | bytes 9437184 | tf_op jit(solution)/shard_map/all_to_all | solution.py:52
  88.2 0.1 copy.35
  88.3 0.1 copy.36
  88.4 0.7 reshape_reshape.7
  89.1 0.6 dynamic_slice.3
  89.8 108.3 %all-to-all-done.1 = bf16[384,32,192]{0,2,1:T(8,128)(2,1)} async-done(((bf16[384,32,192]{0,2,1:T(8,128)(2,1)}), bf16[384,32,192]{0,2,1:T(8,128)(2,1)}, u32[]{:S(2)}, u32[]{:S(2)}) %all-to-all-start.1) | async-done | bytes 4718624 | tf_op jit(solution)/shard_map/all_to_all | solution.py:52
  198.0 5.3 %copy.39 = bf16[32,24,8,384]{3,2,0,1:T(8,128)(2,1)} copy(bf16[32,24,8,384]{3,2,1,0:T(8,128)(2,1)} %bitcast.8) | data formatting | bytes 9437184 | tf_op jit(solution)/shard_map/all_to_all | solution.py:52
  (8 shorter events, 0.0 us)
Async XLA Ops:
  0.6 27.4 %copy-start = (bf16[64,6144]{1,0:T(8,128)(2,1)S(1)}, bf16[64,6144]{1,0:T(8,128)(2,1)}, u32[]{:S(2)}) copy-start(bf16[64,6144]{1,0:T(8,128)(2,1)} %param.7) | copy-start | bytes 2359300
  23.8 12.3 %all-to-all-start.4 = ((bf16[4,2,768]{2,1,0:T(2,128)(2,1)}), bf16[4,2,768]{2,1,0:T(2,128)(2,1)S(1)}, u32[]{:S(2)}, u32[]{:S(2)}) async-start(bf16[4,2,768]{2,1,0:T(2,128)(2,1)} %reshape.22), calls=%async_computation.4 | async-start | bytes 24576 | tf_op jit(solution)/shard_map/all_to_all | solution.py:33
  37.4 22.9 %all-to-all-start = ((f32[32,1,6144]{2,1,0:T(1,128)}), f32[32,1,6144]{2,1,0:T(1,128)S(1)}, u32[]{:S(2)}, u32[]{:S(2)}) async-start(f32[32,1,6144]{2,1,0:T(1,128)} %broadcast_in_dim.4), calls=%async_computation | async-start | bytes 1572864 | tf_op jit(solution)/shard_map/all_to_all | solution.py:16
  60.3 22.8 %all-to-all-start.5 = ((bf16[2,128,48]{1,2,0:T(8,128)(2,1)}), bf16[2,128,48]{1,2,0:T(8,128)(2,1)S(1)}, u32[]{:S(2)}, u32[]{:S(2)}) async-start(bf16[2,128,48]{1,2,0:T(8,128)(2,1)} %pad_maximum_fusion), calls=%async_computation.5 | async-start | bytes 49152 | tf_op jit(solution)/shard_map/all_to_all | solution.py:33
  83.1 114.9 %all-to-all-start.1 = ((bf16[384,32,192]{0,2,1:T(8,128)(2,1)}), bf16[384,32,192]{0,2,1:T(8,128)(2,1)}, u32[]{:S(2)}, u32[]{:S(2)}) async-start(bf16[384,32,192]{0,2,1:T(8,128)(2,1)} %bitcast.14), calls=%async_computation.1 | async-start | bytes 9437184 | tf_op jit(solution)/shard_map/all_to_all | solution.py:52
